TPU v7x, 32 devices: a whole 2x2x4 slice. The times are simulated.
32 devices in a mesh: dp: 4 (over x, core), ctx: 8 (over z, y).
Axes of the slice: x: 2, y: 2, z: 4, core: 2. Of those that a mesh axis runs over, the one named last changes fastest.
Arguments:
- tokens: bfloat16 [4, 4096, 2048], P('dp', 'ctx'), may hold values from -6 to 6
- in_weight: bfloat16 [2048, 5120], P(None, 'dp'), may hold values from -0.125 to 0.125
- step_weight: bfloat16 [2048, 64], replicated, may hold values from -0.125 to 0.125
- step_bias: float32 [64], replicated, may hold values from -3 to 0
- decay_rate: float32 [64], replicated, may hold values from 0.0001 to 0.5
- skip_gain: float32 [64], replicated, may hold values from 0.5 to 1.5
- filter_taps: float32 [4, 5120], replicated, may hold values from -3 to 3
- filter_bias: float32 [5120], replicated, may hold values from -3 to 3
- norm_gain: float32 [4096], replicated, may hold values from 0.5 to 1.5
Outputs:
- normed: bfloat16 [4, 4096, 4096], P('dp', 'ctx')
All inputs are finite; a program needn't handle non-finite values.
Results may differ from a plain program's by a relative error of at most 0.0061.
Values may be sent and summed in bfloat16 or wider, within the bound.
A program may use at most 192 MiB of HBM per device.

v0:
```python
import math
import jax
import jax.numpy as jnp
from jax import lax
from jax.sharding import PartitionSpec as P

HEADS = 64
HEAD_DIM = 64
STATE = 128
GROUPS = 4
BLOCK = 256
GROUP_HEADS = 16


def shifted(value, axis, steps):
    count = lax.axis_size(axis)
    initial, last = (max(0, -steps), min(count, count - steps))
    return lax.ppermute(value, axis, [(source, source + steps) for source in range(initial, last)])


def filter_rows(prefix, current, filter_taps, filter_bias):
    padded = jnp.concatenate([prefix, current], axis=0).astype(jnp.float32)
    length = current.shape[0]
    summed = filter_bias + filter_taps[0] * padded[0:length]
    for offset in range(1, filter_taps.shape[0]):
        summed = summed + filter_taps[offset] * padded[offset : offset + length]
    return summed


def ssd_group(values, input_map, output_map, step_size, decay_rate, skip_gain, block_len):
    length, head_count, head_width = values.shape
    block_count = length // block_len
    bundle = math.gcd(block_count, 8)
    bundle_count = block_count // bundle
    highest = lax.Precision.HIGHEST
    value_rows = values.reshape(block_count, block_len, head_count, head_width)
    input_rows = input_map.reshape(block_count, block_len, -1)
    output_rows = output_map.reshape(block_count, block_len, -1)
    step_rows = step_size.reshape(block_count, block_len, head_count)
    decay_sum = jnp.cumsum(-step_rows * decay_rate, axis=1)
    causal = (jnp.arange(block_len)[:, None] >= jnp.arange(block_len)[None, :])[None, :, :, None]

    def local_block(pieces):
        value_block, input_block, output_block, step_block, decay_block = pieces
        scores = jnp.einsum(
            "ktn,kun->ktu", output_block, input_block, preferred_element_type=jnp.float32
        )
        decay_gap = jnp.where(causal, decay_block[:, :, None, :] - decay_block[:, None, :, :], 0.0)
        weights = (
            jnp.where(causal, jnp.exp(decay_gap), 0.0)
            * scores[..., None]
            * step_block[:, None, :, :]
        ).astype(jnp.bfloat16)
        within = jnp.einsum(
            "ktuh,kuhp->kthp", weights, value_block, preferred_element_type=jnp.float32
        )
        to_end = jnp.exp(decay_block[:, -1:, :] - decay_block) * step_block
        scaled = (to_end[..., None] * value_block.astype(jnp.float32)).astype(jnp.bfloat16)
        states = jnp.einsum(
            "kuhp,kun->khpn", scaled, input_block, preferred_element_type=jnp.float32
        )
        return (within, states)

    def blocked(array):
        return array.reshape((bundle_count, bundle) + array.shape[1:])

    within, states = lax.map(
        local_block,
        (
            blocked(value_rows),
            blocked(input_rows),
            blocked(output_rows),
            blocked(step_rows),
            blocked(decay_sum),
        ),
    )
    within = within.reshape(block_count, block_len, head_count, head_width)
    states = states.reshape((block_count,) + states.shape[2:])
    totals = decay_sum[:, -1, :]
    running = jnp.cumsum(totals, axis=0)
    starts = running - totals
    before = (jnp.arange(block_count)[:, None] > jnp.arange(block_count)[None, :])[:, :, None]
    mixing = jnp.where(
        before, jnp.exp(jnp.where(before, starts[:, None, :] - running[None, :, :], 0.0)), 0.0
    )
    entering = jnp.einsum("kjh,jhpn->khpn", mixing, states, precision=highest)
    carried = (
        jnp.einsum("khpn,ktn->kthp", entering, output_rows.astype(jnp.float32), precision=highest)
        * jnp.exp(decay_sum)[..., None]
    )
    output = within + carried + skip_gain[:, None] * value_rows.astype(jnp.float32)
    return output.reshape(length, head_count, head_width)


def group_norm(values, norm_gain):
    length = values.shape[0]
    grouped = values.astype(jnp.float32).reshape(length, GROUPS, -1)
    mean_square = jnp.mean(jnp.square(grouped), axis=-1, keepdims=True)
    return (grouped * lax.rsqrt(mean_square + 1e-05)).reshape(length, -1) * norm_gain


def sequence_filter(projected, filter_taps, filter_bias):
    reach_rows = filter_taps.shape[0] - 1
    length = projected.shape[0]
    rim_rows = shifted(projected[length - reach_rows :], "ctx", 1)
    return jax.nn.silu(filter_rows(rim_rows, projected, filter_taps, filter_bias)).astype(
        jnp.bfloat16
    )


def head_layout(source, step_raw, step_bias, decay_rate, skip_gain):
    context_size = lax.axis_size("ctx")
    device = lax.axis_index("ctx")
    length = source.shape[0]
    inner_width = HEADS * HEAD_DIM
    local_heads = HEADS // context_size
    local_width = local_heads * HEAD_DIM
    group_share = max(1, GROUP_HEADS // local_heads)
    local_groups = max(1, local_heads // GROUP_HEADS)
    value_parts = source[:, :inner_width].reshape(length, context_size, local_width)
    map_parts = source[:, inner_width:].reshape(length, 2, GROUPS, STATE)
    map_parts = jnp.repeat(map_parts, group_share, axis=2)
    step_parts = step_raw.reshape(length, context_size, local_heads)
    moved_values, moved_input, moved_output, moved_steps = (
        lax.all_to_all(value_parts, "ctx", split_axis=1, concat_axis=0, tiled=True),
        lax.all_to_all(map_parts[:, 0], "ctx", split_axis=1, concat_axis=0, tiled=True),
        lax.all_to_all(map_parts[:, 1], "ctx", split_axis=1, concat_axis=0, tiled=True),
        lax.all_to_all(step_parts, "ctx", split_axis=1, concat_axis=0, tiled=True),
    )
    full_length = moved_values.shape[0]
    head_values = moved_values.reshape(full_length, local_width)
    input_maps = moved_input.reshape(full_length, local_groups * STATE)
    output_maps = moved_output.reshape(full_length, local_groups * STATE)
    bias_slice = lax.dynamic_slice_in_dim(step_bias, device * local_heads, local_heads, 0)
    rate_slice = lax.dynamic_slice_in_dim(decay_rate, device * local_heads, local_heads, 0)
    skip_slice = lax.dynamic_slice_in_dim(skip_gain, device * local_heads, local_heads, 0)
    step_size = jax.nn.softplus(
        moved_steps.reshape(full_length, local_heads).astype(jnp.float32) + bias_slice
    )
    inputs = head_values.reshape(full_length, local_heads, HEAD_DIM)
    pieces = ssd_group(inputs, input_maps, output_maps, step_size, rate_slice, skip_slice, BLOCK)
    mixed_rows = pieces.reshape(full_length, local_width).astype(jnp.bfloat16)
    return lax.all_to_all(mixed_rows, "ctx", split_axis=0, concat_axis=1, tiled=True)


def per_device(
    tokens,
    in_weight,
    step_weight,
    step_bias,
    decay_rate,
    skip_gain,
    filter_taps,
    filter_bias,
    norm_gain,
):
    token_rows = tokens[0]
    projected = jnp.dot(
        token_rows,
        lax.all_gather(in_weight, "dp", axis=1, tiled=True),
        preferred_element_type=jnp.float32,
    ).astype(jnp.bfloat16)
    step_raw = jnp.dot(token_rows, step_weight, preferred_element_type=jnp.float32).astype(
        jnp.bfloat16
    )
    active = sequence_filter(projected, filter_taps, filter_bias)
    mixed_rows = head_layout(active, step_raw, step_bias, decay_rate, skip_gain)
    return group_norm(mixed_rows, norm_gain).astype(jnp.bfloat16)[None]


def solution(mesh):
    in_specs = (P("dp", "ctx", None), P(None, "dp"), P(), P(), P(), P(), P(), P(), P())
    out_specs = P("dp", "ctx", None)
    return jax.shard_map(
        per_device, mesh=mesh, in_specs=in_specs, out_specs=out_specs, check_vma=False
    )
```

profile of v0, /device:TPU:0, one launch (start us, length us, event | category | flops | bytes accessed | tf_op | source)
XLA Modules:
  0.0 554.3 jit_solution(2078704967498910302)
XLA Ops:
  7.3 0.9 copy-done
  8.1 2.3 fusion.45
  10.5 7.3 %all-to-all-start.1 = ((bf16[512,8,8]{0,2,1:T(8,128)(2,1)}), bf16[512,8,8]{0,2,1:T(8,128)(2,1)S(1)}, u32[]{:S(2)}, u32[]{:S(2)}) async-start(bf16[512,8,8]{0,2,1:T(8,128)(2,1)} %fusion.45), calls=%async_computation.1 | async-start | bytes 131072 | tf_op jit(solution)/shard_map/all_to_all | solution.py:128
  17.8 125.4 %all-gather.2.cloned.1.call-done = bf16[2048,5120]{1,0:T(8,128)(2,1)} async-done(((bf16[2048,1280]{1,0:T(8,128)(2,1)}), bf16[2048,5120]{1,0:T(8,128)(2,1)}) %all-gather.2.cloned.1.call-update) | async-done | bytes 20971536 | tf_op jit(solution)/shard_map/all_gather | solution.py:160
  143.2 15.2 %convolution_convert_fusion = bf16[512,5120]{1,0:T(8,128)(2,1)S(1)} fusion(bf16[2048,5120]{1,0:T(8,128)(2,1)} %all-gather.2.cloned.1.call-done, bf16[1,512,2048]{2,1,0:T(8,128)(2,1)S(1)} %copy-done), kind=kOutput, calls=%fused_computation.49 | convolution fusion | flops 10740039680 | bytes 28311552 | tf_op jit(solution)/shard_map/dot_general | solution.py:158
  158.4 3.4 collective-permute-start
  161.9 1.6 collective-permute-done
  163.5 1.5 maximum_convert_fusion
  165.0 6.7 %multiply_convert_fusion.8 = bf16[512,5120]{1,0:T(8,128)(2,1)S(1)} fusion(f32[515,5120]{1,0:T(8,128)S(1)} %maximum_convert_fusion, f32[5120]{0:T(1024)S(1)} %bitcast.192, f32[5120]{0:T(1024)S(1)} %bitcast.193, f32[5120]{0:T(1024)S(1)} %bitcast.191, f32[5120]{0:T(1024)S(1)} %bitcast.190, f32[5120]{0:T(1024)S(1)} %copy-done.7), kind=kLoop, calls=%fused_computation.40 | loop fusion | flops 34078720 | bytes 47288320 | tf_op jit(solution)/shard_map/convert_element_type | solution.py:106
  171.8 2.3 copy-done.5
  174.1 0.8 reshape.188
  175.5 1.6 slice_bitcast_fusion.1
  177.0 6.4 %all-to-all-start.2 = ((bf16[512,8,128]{2,0,1:T(8,128)(2,1)}), bf16[512,8,128]{2,0,1:T(8,128)(2,1)}, u32[]{:S(2)}, u32[]{:S(2)}) async-start(bf16[512,8,128]{2,0,1:T(8,128)(2,1)} %get-tuple-element.173), calls=%async_computation.2 | async-start | bytes 2097152 | tf_op jit(solution)/shard_map/all_to_all | solution.py:127
  183.4 4.7 slice.75
  188.1 6.5 %copy.167 = bf16[512,4096]{0,1:T(8,128)(2,1)} copy(bf16[512,4096]{1,0:T(8,128)(2,1)} %slice.75) | data formatting | bytes 8388608 | tf_op jit(solution)/shard_map/reshape | solution.py:120
  194.6 14.2 %all-to-all-done.2 = bf16[512,8,128]{2,0,1:T(8,128)(2,1)} async-done(((bf16[512,8,128]{2,0,1:T(8,128)(2,1)}), bf16[512,8,128]{2,0,1:T(8,128)(2,1)}, u32[]{:S(2)}, u32[]{:S(2)}) %all-to-all-start.2) | async-done | bytes 1048608 | tf_op jit(solution)/shard_map/all_to_all | solution.py:127
  208.8 4.6 all-to-all-start
  214.2 91.4 %all-to-all-done = bf16[512,8,512]{0,2,1:T(8,128)(2,1)} async-done(((bf16[512,8,512]{0,2,1:T(8,128)(2,1)}), bf16[512,8,512]{0,2,1:T(8,128)(2,1)}, u32[]{:S(2)}, u32[]{:S(2)}) %all-to-all-start) | async-done | bytes 4194336 | tf_op jit(solution)/shard_map/all_to_all | solution.py:125
  305.6 4.7 all-to-all-start.3
  310.5 9.0 %reduce-window.6 = f32[16,8,2,128]{3,1,2,0:T(8,128)S(1)} reduce-window(f32[16,8,2,128]{3,1,2,0:T(8,128)S(1)} %fusion.50, f32[]{:T(128)} %constant.30.clone.1), window={size=1x1x1x128 pad=0_0x0_0x0_0x127_0}, to_apply=%region_0.1 | reduce-window | flops 4161536 | bytes 262148 | tf_op jit(solution)/shard_map/reduce-window
  321.5 6.5 %copy.143 = bf16[8,512,1,512]{1,0,3,2:T(8,128)(2,1)} copy(bf16[8,512,1,512]{1,3,0,2:T(8,128)(2,1)} %bitcast.7) | data formatting | bytes 8388608 | tf_op jit(solution)/shard_map/all_to_all | solution.py:125
  327.9 7.1 %reshape_reshape_reshape_reshape.3 = bf16[2,8,256,8,64]{2,1,0,4,3:T(8,128)(2,1)} reshape(bf16[8,512,1,512]{1,0,3,2:T(8,128)(2,1)} %copy.143) | data formatting | bytes 8388608 | tf_op jit(solution)/shard_map/reshape;reshape;reshape;reshape | solution.py:65
  335.0 0.9 all-to-all-done.3
  335.9 34.5 %while.14 = (s32[]{:T(128)}, f32[2,8,256,8,64]{2,4,3,1,0:T(8,128)}, f32[2,8,8,64,128]{4,3,2,1,0:T(8,128)}, bf16[2,8,256,8,64]{2,1,0,4,3:T(8,128)(2,1)}, f32[2,8,...) while((s32[]{:T(128)}, f32[2,8,256,8,64]{2,4,3,1,0:T(8,128)}, ...), condition=%wide.region_3.4_spmd.clone.clone, body=%wide.region_2.3_spmd.clone.clone.sunk | while | flops 967933952 | bytes 30084480 | solution.py:67
  335.9 1.6 fusion.77
  337.6 1.7 constant_dynamic-slice_fusion.6
  339.4 1.3 copy-done.2
  340.6 7.4 %bitcast_dynamic-update-slice_fusion.4 = f32[2,8,256,8,64]{2,4,3,1,0:T(8,128)} fusion(f32[2,8,256,8,64]{2,4,3,1,0:T(8,128)} %get-tuple-element.241, s32[]{:T(128)} %get-tuple-element.240, f32[8,256,8]{1,2,0:T(8,128)S(1)} %bitcast.182, f32[8,256,256]{2,1,0:T(8,128)S(1)} %fusion.77, f32[8,256,8]{1,2,0:T(8,128)S(1)} %bitcast.183, ...), kind=kOutput, calls=%fused_computation.9.clone.1 | convolution fusion | flops 562036736 | bytes 8651264 | tf_op jit(solution)/shard_map/while/body/eval_jaxpr/ktuh,kuhp->kthp/dot_general | solution.py:54
  349.4 3.7 bitcast_dynamic-update-slice_fusion.5
  353.1 1.6 fusion.77
  354.8 1.7 constant_dynamic-slice_fusion.6
  356.6 1.3 copy-done.2
  357.9 7.4 %bitcast_dynamic-update-slice_fusion.4 = f32[2,8,256,8,64]{2,4,3,1,0:T(8,128)} fusion(f32[2,8,256,8,64]{2,4,3,1,0:T(8,128)} %get-tuple-element.241, s32[]{:T(128)} %get-tuple-element.240, f32[8,256,8]{1,2,0:T(8,128)S(1)} %bitcast.182, f32[8,256,256]{2,1,0:T(8,128)S(1)} %fusion.77, f32[8,256,8]{1,2,0:T(8,128)S(1)} %bitcast.183, ...), kind=kOutput, calls=%fused_computation.9.clone.1 | convolution fusion | flops 562036736 | bytes 8651264 | tf_op jit(solution)/shard_map/while/body/eval_jaxpr/ktuh,kuhp->kthp/dot_general | solution.py:54
  366.7 3.7 bitcast_dynamic-update-slice_fusion.5
  370.4 3.4 bitcast_convert_fusion.1
  373.8 8.1 %copy.158 = f32[8,512,1,512]{1,0,3,2:T(8,128)} copy(f32[8,512,1,512]{1,3,0,2:T(8,128)S(1)} %bitcast_convert_fusion.1) | data formatting | bytes 16777216 | tf_op jit(solution)/shard_map/convert_element_type | solution.py:91
  381.8 9.5 %reshape.194 = f32[16,256,8,64]{1,0,3,2:T(8,128)} reshape(f32[8,512,1,512]{1,0,3,2:T(8,128)} %copy.158) | data formatting | bytes 16777216 | tf_op jit(solution)/shard_map/convert_element_type | solution.py:91
  391.3 10.2 %fusion.36 = f32[16,8,64,128]{3,0,2,1:T(8,128)} fusion(f32[16,8,64,128]{3,2,1,0:T(8,128)} %bitcast.186, f32[16,8]{0,1:T(8,128)S(1)} %copy.153, f32[16,8]{0,1:T(8,128)S(1)} %fusion.62, pred[16,16]{1,0:T(8,128)(4,1)S(1)} %iota_compare_fusion.1), kind=kOutput, calls=%fused_computation.55 | convolution fusion | flops 201332736 | bytes 8389888 | tf_op jit(solution)/shard_map/kjh,jhpn->khpn/dot_general | solution.py:86
  401.6 15.8 %fusion.29 = bf16[16,256,8,64]{1,3,2,0:T(8,128)(2,1)} fusion(f32[2,8,256,8,64]{2,4,3,1,0:T(8,128)} %get-tuple-element.56, f32[16,256,8,64]{1,0,3,2:T(8,128)S(1)} %copy-done.4, f32[8]{0:T(128)S(1)} %copy-done.9, f32[16,256,8]{1,2,0:T(8,128)S(1)} %copy.157, bf16[16,256,128,1]{2,1,3,0:T(8,128)(2,1)} %bitcast.34, f32[16,8,64,128]{3,0,2,1:T(8,128)} %fusion.36), kind=kOutput, calls=%fused_computation.46 | convolution fusion | flops 3231711232 | bytes 26345504 | tf_op jit(solution)/shard_map/khpn,ktn->kthp/dot_general | solution.py:88
  417.4 6.7 %copy.160 = bf16[16,256,8,64]{1,0,3,2:T(8,128)(2,1)} copy(bf16[16,256,8,64]{1,3,2,0:T(8,128)(2,1)} %fusion.29) | data formatting | bytes 8388608 | tf_op jit(solution)/shard_map/convert_element_type | solution.py:142
  424.1 7.1 %convert_element_type.101 = bf16[8,512,512]{1,0,2:T(8,128)(2,1)} reshape(bf16[16,256,8,64]{1,0,3,2:T(8,128)(2,1)} %copy.160) | data formatting | bytes 8388608 | tf_op jit(solution)/shard_map/convert_element_type | solution.py:142
  431.2 3.6 copy.161
  434.8 97.4 %all_to_all.64 = bf16[8,512,512]{1,2,0:T(8,128)(2,1)S(1)} all-to-all(bf16[8,512,512]{1,2,0:T(8,128)(2,1)S(1)} %copy.161), channel_id=1, replica_groups=mesh['dp'=4,'ctx'=8] {'ctx'}, dimensions={0} | all-to-all | bytes 8388608 | tf_op jit(solution)/shard_map/all_to_all | solution.py:143
  532.2 2.0 copy-done.3
  534.2 0.8 multiply_reduce_fusion
  535.1 3.3 convert_element_type.116
  538.5 2.4 fusion.27
  540.9 6.3 %copy.163 = bf16[1,512,4096]{2,1,0:T(8,128)(2,1)} copy(bf16[1,512,4096]{1,2,0:T(8,128)(2,1)} %fusion.27) | data formatting | bytes 8388608 | tf_op jit(solution)/shard_map/convert_element_type | solution.py:168
  (72 shorter events, 7.0 us)
Async XLA Ops:
  6.5 1.6 copy-start
  6.5 136.7 %all-gather.2.cloned.1.call-start = ((), (), s32[]{:S(2)}) async-start(), calls=%async_computation.5 | async-start | bytes 26214400 | tf_op jit(solution)/shard_map/all_gather | solution.py:160
  10.5 166.6 %all-to-all-start.1 = ((bf16[512,8,8]{0,2,1:T(8,128)(2,1)}), bf16[512,8,8]{0,2,1:T(8,128)(2,1)S(1)}, u32[]{:S(2)}, u32[]{:S(2)}) async-start(bf16[512,8,8]{0,2,1:T(8,128)(2,1)} %fusion.45), calls=%async_computation.1 | async-start | bytes 131072 | tf_op jit(solution)/shard_map/all_to_all | solution.py:128
  17.8 144.0 %copy-start.6 = (f32[4,5120]{1,0:T(4,128)S(1)}, f32[4,5120]{1,0:T(4,128)}, u32[]{:S(2)}) copy-start(f32[4,5120]{1,0:T(4,128)} %param.17) | copy-start | bytes 245764
  158.4 6.6 %copy-start.7 = (f32[5120]{0:T(1024)S(1)}, f32[5120]{0:T(1024)}, u32[]{:S(2)}) copy-start(f32[5120]{0:T(1024)} %param.18) | copy-start | bytes 61444
  158.4 5.0 collective-permute-start
  171.8 2.3 copy-start.5
  177.0 31.7 %all-to-all-start.2 = ((bf16[512,8,128]{2,0,1:T(8,128)(2,1)}), bf16[512,8,128]{2,0,1:T(8,128)(2,1)}, u32[]{:S(2)}, u32[]{:S(2)}) async-start(bf16[512,8,128]{2,0,1:T(8,128)(2,1)} %get-tuple-element.173), calls=%async_computation.2 | async-start | bytes 2097152 | tf_op jit(solution)/shard_map/all_to_all | solution.py:127
  188.1 25.3 %copy-start.10 = (f32[64]{0:T(128)S(1)}, f32[64]{0:T(128)}, u32[]{:S(2)}) copy-start(f32[64]{0:T(128)} %param.14) | copy-start | bytes 772
  188.1 25.4 %copy-start.11 = (f32[64]{0:T(128)S(1)}, f32[64]{0:T(128)}, u32[]{:S(2)}) copy-start(f32[64]{0:T(128)} %param.15) | copy-start | bytes 772
  188.1 25.4 %copy-start.12 = (f32[64]{0:T(128)S(1)}, f32[64]{0:T(128)}, u32[]{:S(2)}) copy-start(f32[64]{0:T(128)} %param.16) | copy-start | bytes 772
  208.8 96.8 %all-to-all-start = ((bf16[512,8,512]{0,2,1:T(8,128)(2,1)}), bf16[512,8,512]{0,2,1:T(8,128)(2,1)}, u32[]{:S(2)}, u32[]{:S(2)}) async-start(bf16[512,8,512]{0,2,1:T(8,128)(2,1)} %bitcast.180), calls=%async_computation | async-start | bytes 8388608 | tf_op jit(solution)/shard_map/all_to_all | solution.py:125
  305.6 30.3 %all-to-all-start.3 = ((bf16[512,8,128]{2,0,1:T(8,128)(2,1)}), bf16[512,8,128]{2,0,1:T(8,128)(2,1)}, u32[]{:S(2)}, u32[]{:S(2)}) async-start(bf16[512,8,128]{2,0,1:T(8,128)(2,1)} %get-tuple-element.172), calls=%async_computation.3 | async-start | bytes 2097152 | tf_op jit(solution)/shard_map/all_to_all | solution.py:126
  339.3 1.3 copy-start.2
  356.5 1.3 copy-start.2
  391.3 10.3 %copy-start.4 = (f32[16,256,8,64]{1,0,3,2:T(8,128)S(1)}, f32[16,256,8,64]{1,0,3,2:T(8,128)}, u32[]{:S(2)}) copy-start(f32[16,256,8,64]{1,0,3,2:T(8,128)} %reshape.194) | copy-start | bytes 25165828
  391.3 10.3 %copy-start.9 = (f32[8]{0:T(128)S(1)}, f32[8]{0:T(128)}, u32[]{:S(2)}) copy-start(f32[8]{0:T(128)} %dynamic_slice.29) | copy-start | bytes 100
  532.2 2.0 copy-start.3
  534.2 4.3 copy-start.8
  538.5 8.8 %copy-start.1 = (bf16[1,512,2048]{2,1,0:T(8,128)(2,1)S(1)}, bf16[1,512,2048]{2,1,0:T(8,128)(2,1)}, u32[]{:S(2)}) copy-start(bf16[1,512,2048]{2,1,0:T(8,128)(2,1)} %param.11) | copy-start | bytes 6291460
Sparse Core Ops, SparseCore 0:
  8.9 134.2 all-gather.1
where the time goes:
time: 563 us; the launch traced here: 554 us
  waiting for transfers between devices  234 us (42%)
  blocking collectives  97.4 us (17%)
  local copies, waits for them, and re-layouts  84.9 us (15%)
  matrix products  69.2 us (12%)
  other arithmetic  28.3 us (5%)
  starting transfers between devices  26.3 us (5%)
  between operations  14 us (2%)
    all_gather x1, waiting for transfers between devices, per_device(): lax.all_gather(in_weight, 'dp', axis=1, tiled=True)  125 us
    all_to_all x1, blocking collectives, head_layout(): lax.all_to_all(mixed_rows, 'ctx', split_axis=0, concat_axis=1, tiled=True)  97.4 us
    all_to_all x1, waiting for transfers between devices, head_layout(): lax.all_to_all(value_parts, 'ctx', split_axis=1, concat_axis=0, tiled=True)  91.4 us
    convert_element_type x2, local copies, waits for them, and re-layouts, ssd_group(): value_rows.astype(jnp.float32)  17.6 us
    convert_element_type x3, local copies, waits for them, and re-layouts, head_layout(): mixed_rows = pieces.reshape(full_length, local_width).astype(jnp.bfloat16)  17.4 us
    dot_general x1, matrix products, ssd_group(): jnp.einsum('khpn,ktn->kthp', entering, output_rows.astype(jnp.float32), p...  15.8 us
    dot_general x1, matrix products, per_device(): jnp.dot(token_rows, lax.all_gather(in_weight, 'dp', axis=1, tiled=True),...  15.2 us
    dot_general x2, matrix products, local_block(): jnp.einsum('ktuh,kuhp->kthp', weights, value_block, preferred_element_typ...  14.9 us
  transfers between devices with their start and end apart: 6, of which 5 were waited for; matrix products, arithmetic and copies ran while one was open for 12% of the time, Pallas kernels for 0%

commit v1 on v0

--- a/solution.py
+++ b/solution.py
@@ -122,7 +122,12 @@
     map_parts = jnp.repeat(map_parts, group_share, axis=2)
     step_parts = step_raw.reshape(length, context_size, local_heads)
     moved_values, moved_input, moved_output, moved_steps = (
-        lax.all_to_all(value_parts, "ctx", split_axis=1, concat_axis=0, tiled=True),
+        jnp.concatenate(
+            lax.all_to_all(
+                jnp.stack(jnp.split(value_parts, lax.axis_size("ctx"), axis=1)), "ctx", 0, 0
+            ),
+            axis=0,
+        ),
         lax.all_to_all(map_parts[:, 0], "ctx", split_axis=1, concat_axis=0, tiled=True),
         lax.all_to_all(map_parts[:, 1], "ctx", split_axis=1, concat_axis=0, tiled=True),
         lax.all_to_all(step_parts, "ctx", split_axis=1, concat_axis=0, tiled=True),

time: 563 us -> 588 us (1.044)
  local copies, waits for them, and re-layouts: 84.9 us -> 121 us
    unnamed x24 -> x41, local copies, waits for them, and re-layouts: 5.23 us -> 29.8 us
    split x0 -> x1, local copies, waits for them, and re-layouts: none -> 22.4 us  [head_layout(): jnp.split(value_parts, lax.axis_size('ctx'), axis=1)]
    all_to_all x1, waiting for transfers between devices: 14.2 us -> 0.01 us  [head_layout(): lax.all_to_all(map_parts[:, 1], 'ctx', split_axis=1, concat_axis=0, tiled...]
    all_to_all x1, waiting for transfers between devices: 0.86 us -> 12.9 us  [head_layout(): lax.all_to_all(map_parts[:, 0], 'ctx', split_axis=1, concat_axis=0, tiled...]
    convert_element_type x2, local copies, waits for them, and re-layouts: 17.6 us -> 24.8 us  [ssd_group(): value_rows.astype(jnp.float32)]
    reshape x1 -> x0, local copies, waits for them, and re-layouts: 6.5 us -> none  [head_layout(): source[:, :inner_width].reshape(length, context_size, local_width)]
    all_to_all x1 -> x0, local copies, waits for them, and re-layouts: 6.48 us -> none  [head_layout(): lax.all_to_all(value_parts, 'ctx', split_axis=1, concat_axis=0, tiled=True)]
  transfers between devices with their start and end apart: 6 -> 6, of which waited for: 5 -> 4; matrix products, arithmetic and copies ran while one was open for 12% -> 17% of each run, Pallas kernels for 0% -> 0%
where the time goes in v1:
time: 588 us; the launch traced here: 583 us
  waiting for transfers between devices  233 us (40%)
  local copies, waits for them, and re-layouts  121 us (21%)
  blocking collectives  98.3 us (17%)
  matrix products  64.7 us (11%)
  starting transfers between devices  26.7 us (5%)
  other arithmetic  24.9 us (4%)
  between operations  14 us (2%)
    all_gather x1, waiting for transfers between devices, per_device(): lax.all_gather(in_weight, 'dp', axis=1, tiled=True)  126 us
    all_to_all x1, blocking collectives, head_layout(): lax.all_to_all(mixed_rows, 'ctx', split_axis=0, concat_axis=1, tiled=True)  98.3 us
    all_to_all x1, waiting for transfers between devices, head_layout(): lax.all_to_all(jnp.stack(jnp.split(value_parts, lax.axis_size('ctx'), axi...  91.9 us
    unnamed x41, local copies, waits for them, and re-layouts  29.8 us
    convert_element_type x2, local copies, waits for them, and re-layouts, ssd_group(): value_rows.astype(jnp.float32)  24.8 us
    split x1, local copies, waits for them, and re-layouts, head_layout(): jnp.split(value_parts, lax.axis_size('ctx'), axis=1)  22.4 us
    convert_element_type x3, local copies, waits for them, and re-layouts, head_layout(): mixed_rows = pieces.reshape(full_length, local_width).astype(jnp.bfloat16)  17.6 us
    dot_general x1, matrix products, per_device(): jnp.dot(token_rows, lax.all_gather(in_weight, 'dp', axis=1, tiled=True),...  15.2 us
  transfers between devices with their start and end apart: 6, of which 4 were waited for; matrix products, arithmetic and copies ran while one was open for 17% of the time, Pallas kernels for 0%

profile of v1, /device:TPU:0, one launch (start us, length us, event | category | flops | bytes accessed | tf_op | source)
XLA Modules:
  0.0 583.2 jit_solution(6530283085383029566)
XLA Ops:
  8.1 1.4 fusion.50
  9.5 7.3 %all-to-all-start.1 = ((bf16[512,8,8]{0,2,1:T(8,128)(2,1)}), bf16[512,8,8]{0,2,1:T(8,128)(2,1)S(1)}, u32[]{:S(2)}, u32[]{:S(2)}) async-start(bf16[512,8,8]{0,2,1:T(8,128)(2,1)} %fusion.50), calls=%async_computation.1 | async-start | bytes 131072 | tf_op jit(solution)/shard_map/all_to_all | solution.py:133
  16.8 126.4 %all-gather.2.cloned.1.call-done = bf16[2048,5120]{1,0:T(8,128)(2,1)} async-done(((bf16[2048,1280]{1,0:T(8,128)(2,1)}), bf16[2048,5120]{1,0:T(8,128)(2,1)}) %all-gather.2.cloned.1.call-update) | async-done | bytes 20971536 | tf_op jit(solution)/shard_map/all_gather | solution.py:165
  143.2 15.2 %convolution_convert_fusion = bf16[512,5120]{1,0:T(8,128)(2,1)S(1)} fusion(bf16[2048,5120]{1,0:T(8,128)(2,1)} %all-gather.2.cloned.1.call-done, bf16[1,512,2048]{2,1,0:T(8,128)(2,1)S(1)} %copy-done), kind=kOutput, calls=%fused_computation.51 | convolution fusion | flops 10740039680 | bytes 28311552 | tf_op jit(solution)/shard_map/dot_general | solution.py:163
  158.4 3.7 collective-permute-start
  162.2 1.3 collective-permute-done
  163.5 1.5 maximum_convert_fusion
  165.0 6.7 %multiply_convert_fusion.8 = bf16[512,5120]{1,0:T(8,128)(2,1)S(1)} fusion(f32[515,5120]{1,0:T(8,128)S(1)} %maximum_convert_fusion, f32[5120]{0:T(1024)S(1)} %bitcast.223, f32[5120]{0:T(1024)S(1)} %bitcast.224, f32[5120]{0:T(1024)S(1)} %bitcast.222, f32[5120]{0:T(1024)S(1)} %bitcast.221, f32[5120]{0:T(1024)S(1)} %copy-done.14), kind=kLoop, calls=%fused_computation.43 | loop fusion | flops 34078720 | bytes 47288320 | tf_op jit(solution)/shard_map/convert_element_type | solution.py:106
  172.1 1.9 copy-done.5
  174.1 4.3 copy.238
  179.3 22.4 %fusion.77 = (bf16[512,1,512]{2,1,0:T(2,128)(2,1)S(1)}, bf16[512,1,512]{2,1,0:T(2,128)(2,1)}, bf16[512,1,512]{2,1,0:T(2,128)(2,1)}, bf16[512,1,512]{2,1,0:T(2,12...) fusion(bf16[512,8,512]{2,1,0:T(8,128)(2,1)} %bitcast.209), kind=kLoop, calls=%fused_computation.106 | loop fusion | bytes 8388608 | tf_op jit(solution)/shard_map/split | solution.py:127
  202.1 1.5 slice_bitcast_fusion.1
  203.6 6.4 %all-to-all-start.3 = ((bf16[512,8,128]{2,0,1:T(8,128)(2,1)}), bf16[512,8,128]{2,0,1:T(8,128)(2,1)}, u32[]{:S(2)}, u32[]{:S(2)}) async-start(bf16[512,8,128]{2,0,1:T(8,128)(2,1)} %get-tuple-element.180), calls=%async_computation.3 | async-start | bytes 2097152 | tf_op jit(solution)/shard_map/all_to_all | solution.py:131
  210.0 2.3 fusion.60
  212.3 2.2 fusion.59
  214.5 2.1 fusion.58
  216.7 2.2 fusion.57
  218.8 0.9 fusion.56
  219.8 0.9 fusion.55
  220.7 0.9 fusion.54
  221.6 0.9 fusion.53
  222.5 12.9 %all-to-all-done.3 = bf16[512,8,128]{2,0,1:T(8,128)(2,1)} async-done(((bf16[512,8,128]{2,0,1:T(8,128)(2,1)}), bf16[512,8,128]{2,0,1:T(8,128)(2,1)}, u32[]{:S(2)}, u32[]{:S(2)}) %all-to-all-start.3) | async-done | bytes 1048608 | tf_op jit(solution)/shard_map/all_to_all | solution.py:131
  235.4 4.6 all-to-all-start
  240.3 91.9 %all-to-all-done = bf16[8,512,1,512]{3,1,2,0:T(8,128)(2,1)} async-done(((bf16[8,512,1,512]{3,1,2,0:T(8,128)(2,1)}), bf16[8,512,1,512]{3,1,2,0:T(8,128)(2,1)}, u32[]{:S(2)}, u32[]{:S(2)}) %all-to-all-start) | async-done | bytes 4194336 | tf_op jit(solution)/shard_map/all_to_all | solution.py:126
  332.2 4.8 all-to-all-start.2
  337.1 9.0 %reduce-window.6 = f32[16,8,2,128]{3,1,2,0:T(8,128)S(1)} reduce-window(f32[16,8,2,128]{3,1,2,0:T(8,128)S(1)} %fusion.63, f32[]{:T(128)} %constant.30.clone.1), window={size=1x1x1x128 pad=0_0x0_0x0_0x127_0}, to_apply=%region_0.1 | reduce-window | flops 4161536 | bytes 262148 | tf_op jit(solution)/shard_map/reduce-window
  347.5 1.0 copy.210
  348.7 11.2 %reshape.199 = bf16[2,8,256,8,64]{4,3,2,1,0:T(8,128)(2,1)} reshape(bf16[8,512,1,512]{3,1,2,0:T(8,128)(2,1)} %all-to-all-done) | data formatting | bytes 8388608 | tf_op jit(solution)/shard_map/reshape;reshape;reshape;reshape;reshape | solution.py:65
  360.0 9.1 %copy.202 = bf16[2,8,256,8,64]{2,4,3,1,0:T(8,128)(2,1)} copy(bf16[2,8,256,8,64]{4,3,2,1,0:T(8,128)(2,1)} %reshape.199) | data formatting | bytes 8388608
  369.1 28.8 %while.14 = (s32[]{:T(128)}, f32[2,8,256,8,64]{2,4,3,1,0:T(8,128)}, f32[2,8,8,64,128]{4,3,2,1,0:T(8,128)}, bf16[2,8,256,8,64]{2,4,3,1,0:T(8,128)(2,1)}, f32[2,8,...) while((s32[]{:T(128)}, f32[2,8,256,8,64]{2,4,3,1,0:T(8,128)}, ...), condition=%wide.region_3.4_spmd.clone.clone, body=%wide.region_2.3_spmd.clone.clone.sunk | while | flops 967933952 | bytes 35328444 | solution.py:67
  370.7 1.8 fusion.93
  372.5 3.7 bitcast_dynamic-update-slice_fusion.5
  376.2 7.3 %bitcast_dynamic-update-slice_fusion.4 = f32[2,8,256,8,64]{2,4,3,1,0:T(8,128)} fusion(f32[2,8,256,8,64]{2,4,3,1,0:T(8,128)} %get-tuple-element.249, s32[]{:T(128)S(6)} %copy.289, f32[8,256,8]{1,2,0:T(8,128)S(1)} %bitcast.213, f32[8,256,256]{2,1,0:T(8,128)S(1)} %fusion.93, f32[8,256,8]{1,2,0:T(8,128)S(1)} %bitcast.214, ...), kind=kOutput, calls=%fused_computation.9.clone.1 | convolution fusion | flops 562036736 | bytes 8651776 | tf_op jit(solution)/shard_map/while/body/eval_jaxpr/ktuh,kuhp->kthp/dot_general | solution.py:54
  385.1 1.8 fusion.93
  386.9 3.7 bitcast_dynamic-update-slice_fusion.5
  390.6 7.3 %bitcast_dynamic-update-slice_fusion.4 = f32[2,8,256,8,64]{2,4,3,1,0:T(8,128)} fusion(f32[2,8,256,8,64]{2,4,3,1,0:T(8,128)} %get-tuple-element.249, s32[]{:T(128)S(6)} %copy.289, f32[8,256,8]{1,2,0:T(8,128)S(1)} %bitcast.213, f32[8,256,256]{2,1,0:T(8,128)S(1)} %fusion.93, f32[8,256,8]{1,2,0:T(8,128)S(1)} %bitcast.214, ...), kind=kOutput, calls=%fused_computation.9.clone.1 | convolution fusion | flops 562036736 | bytes 8651776 | tf_op jit(solution)/shard_map/while/body/eval_jaxpr/ktuh,kuhp->kthp/dot_general | solution.py:54
  397.9 11.9 %reshape.200 = f32[16,256,8,64]{3,2,1,0:T(8,128)} reshape(bf16[8,512,1,512]{3,1,2,0:T(8,128)(2,1)} %all-to-all-done) | data formatting | bytes 12582912 | tf_op jit(solution)/shard_map/convert_element_type | solution.py:91
  409.8 12.9 %copy.212 = f32[16,256,8,64]{1,3,2,0:T(8,128)} copy(f32[16,256,8,64]{3,2,1,0:T(8,128)} %reshape.200) | data formatting | bytes 16777216 | tf_op jit(solution)/shard_map/convert_element_type | solution.py:91
  422.7 10.2 %fusion.41 = f32[16,8,64,128]{3,0,2,1:T(8,128)} fusion(f32[16,8,64,128]{3,2,1,0:T(8,128)} %bitcast.217, f32[16,8]{0,1:T(8,128)S(1)} %copy.206, f32[16,8]{0,1:T(8,128)S(1)} %fusion.75, pred[16,16]{1,0:T(8,128)(4,1)S(1)} %iota_compare_fusion.1), kind=kOutput, calls=%fused_computation.57 | convolution fusion | flops 201332736 | bytes 8389888 | tf_op jit(solution)/shard_map/kjh,jhpn->khpn/dot_general | solution.py:86
  433.0 12.3 %fusion.34 = bf16[16,256,8,64]{1,3,2,0:T(8,128)(2,1)} fusion(f32[2,8,256,8,64]{2,4,3,1,0:T(8,128)} %get-tuple-element.56, f32[16,256,8,64]{1,3,2,0:T(8,128)S(1)} %copy-done.4, f32[8]{0:T(128)S(1)} %dynamic_slice.29, f32[16,256,8]{1,2,0:T(8,128)S(1)} %copy-done.11, bf16[16,256,128,1]{2,1,3,0:T(8,128)(2,1)} %bitcast.39, f32[16,8,64,128]{3,0,2,1:T(8,128)} %fusion.41), kind=kOutput, calls=%fused_computation.49 | convolution fusion | flops 3231711232 | bytes 26345504 | tf_op jit(solution)/shard_map/khpn,ktn->kthp/dot_general | solution.py:88
  445.2 6.9 %copy.213 = bf16[16,256,8,64]{1,0,3,2:T(8,128)(2,1)} copy(bf16[16,256,8,64]{1,3,2,0:T(8,128)(2,1)} %fusion.34) | data formatting | bytes 8388608 | tf_op jit(solution)/shard_map/convert_element_type | solution.py:147
  452.1 7.1 %convert_element_type.101 = bf16[8,512,512]{1,0,2:T(8,128)(2,1)} reshape(bf16[16,256,8,64]{1,0,3,2:T(8,128)(2,1)} %copy.213) | data formatting | bytes 8388608 | tf_op jit(solution)/shard_map/convert_element_type | solution.py:147
  459.2 3.6 copy.214
  462.8 98.3 %all_to_all.54 = bf16[8,512,512]{1,2,0:T(8,128)(2,1)S(1)} all-to-all(bf16[8,512,512]{1,2,0:T(8,128)(2,1)S(1)} %copy.214), channel_id=1, replica_groups=mesh['dp'=4,'ctx'=8] {'ctx'}, dimensions={0} | all-to-all | bytes 8388608 | tf_op jit(solution)/shard_map/all_to_all | solution.py:148
  561.1 2.0 copy-done.3
  564.0 3.3 convert_element_type.116
  567.4 2.4 fusion.32
  569.8 6.3 %copy.216 = bf16[1,512,4096]{2,1,0:T(8,128)(2,1)} copy(bf16[1,512,4096]{1,2,0:T(8,128)(2,1)} %fusion.32) | data formatting | bytes 8388608 | tf_op jit(solution)/shard_map/convert_element_type | solution.py:173
  (95 shorter events, 9.3 us)
Async XLA Ops:
  6.5 1.6 copy-start
  6.5 1.6 copy-start.12
  6.5 136.7 %all-gather.2.cloned.1.call-start = ((), (), s32[]{:S(2)}) async-start(), calls=%async_computation.5 | async-start | bytes 26214400 | tf_op jit(solution)/shard_map/all_gather | solution.py:165
  9.5 194.1 %all-to-all-start.1 = ((bf16[512,8,8]{0,2,1:T(8,128)(2,1)}), bf16[512,8,8]{0,2,1:T(8,128)(2,1)S(1)}, u32[]{:S(2)}, u32[]{:S(2)}) async-start(bf16[512,8,8]{0,2,1:T(8,128)(2,1)} %fusion.50), calls=%async_computation.1 | async-start | bytes 131072 | tf_op jit(solution)/shard_map/all_to_all | solution.py:133
  16.8 145.3 %copy-start.13 = (f32[4,5120]{1,0:T(4,128)S(1)}, f32[4,5120]{1,0:T(4,128)}, u32[]{:S(2)}) copy-start(f32[4,5120]{1,0:T(4,128)} %param.17) | copy-start | bytes 245764
  158.4 5.0 collective-permute-start
  162.2 2.8 copy-start.14
  171.7 2.3 copy-start.5
  174.1 4.3 slice-start
  203.6 31.7 %all-to-all-start.3 = ((bf16[512,8,128]{2,0,1:T(8,128)(2,1)}), bf16[512,8,128]{2,0,1:T(8,128)(2,1)}, u32[]{:S(2)}, u32[]{:S(2)}) async-start(bf16[512,8,128]{2,0,1:T(8,128)(2,1)} %get-tuple-element.180), calls=%async_computation.3 | async-start | bytes 2097152 | tf_op jit(solution)/shard_map/all_to_all | solution.py:131
  210.0 8.8 %copy-start.8 = (bf16[512,1,512]{2,1,0:T(2,128)(2,1)S(1)}, bf16[512,1,512]{2,1,0:T(2,128)(2,1)}, u32[]{:S(2)}) copy-start(bf16[512,1,512]{2,1,0:T(2,128)(2,1)} %get-tuple-element.175) | copy-start | bytes 1572868
  210.0 9.7 %copy-start.7 = (bf16[512,1,512]{2,1,0:T(2,128)(2,1)S(1)}, bf16[512,1,512]{2,1,0:T(2,128)(2,1)}, u32[]{:S(2)}) copy-start(bf16[512,1,512]{2,1,0:T(2,128)(2,1)} %get-tuple-element.174) | copy-start | bytes 1572868
  212.3 8.4 %copy-start.6 = (bf16[512,1,512]{2,1,0:T(2,128)(2,1)S(1)}, bf16[512,1,512]{2,1,0:T(2,128)(2,1)}, u32[]{:S(2)}) copy-start(bf16[512,1,512]{2,1,0:T(2,128)(2,1)} %get-tuple-element.173) | copy-start | bytes 1572868
  222.5 17.5 %copy-start.16 = (f32[64]{0:T(128)S(1)}, f32[64]{0:T(128)}, u32[]{:S(2)}) copy-start(f32[64]{0:T(128)} %param.14) | copy-start | bytes 772
  222.5 17.6 %copy-start.17 = (f32[64]{0:T(128)S(1)}, f32[64]{0:T(128)}, u32[]{:S(2)}) copy-start(f32[64]{0:T(128)} %param.15) | copy-start | bytes 772
  222.5 17.7 %copy-start.18 = (f32[64]{0:T(128)S(1)}, f32[64]{0:T(128)}, u32[]{:S(2)}) copy-start(f32[64]{0:T(128)} %param.16) | copy-start | bytes 772
  235.4 96.8 %all-to-all-start = ((bf16[8,512,1,512]{3,1,2,0:T(8,128)(2,1)}), bf16[8,512,1,512]{3,1,2,0:T(8,128)(2,1)}, u32[]{:S(2)}, u32[]{:S(2)}) async-start(bf16[8,512,1,512]{3,1,2,0:T(8,128)(2,1)} %fusion.53), calls=%async_computation | async-start | bytes 8388608 | tf_op jit(solution)/shard_map/all_to_all | solution.py:126
  332.2 36.9 %all-to-all-start.2 = ((bf16[512,8,128]{2,0,1:T(8,128)(2,1)}), bf16[512,8,128]{2,0,1:T(8,128)(2,1)}, u32[]{:S(2)}, u32[]{:S(2)}) async-start(bf16[512,8,128]{2,0,1:T(8,128)(2,1)} %get-tuple-element.181), calls=%async_computation.2 | async-start | bytes 2097152 | tf_op jit(solution)/shard_map/all_to_all | solution.py:132
  369.1 0.6 copy-start.9
  370.7 5.5 copy-start.2
  376.2 7.3 %copy-start.10 = (f32[2,8,256,8]{2,3,1,0:T(8,128)S(1)}, f32[2,8,256,8]{2,3,1,0:T(8,128)}, u32[]{:S(2)}) copy-start(f32[2,8,256,8]{2,3,1,0:T(8,128)} %copy-done.9) | copy-start | bytes 393220 | tf_op jit(solution)/shard_map/while
  383.5 0.6 copy-start.9
  385.1 5.5 copy-start.2
  390.6 7.3 %copy-start.10 = (f32[2,8,256,8]{2,3,1,0:T(8,128)S(1)}, f32[2,8,256,8]{2,3,1,0:T(8,128)}, u32[]{:S(2)}) copy-start(f32[2,8,256,8]{2,3,1,0:T(8,128)} %copy-done.9) | copy-start | bytes 393220 | tf_op jit(solution)/shard_map/while
  409.8 23.2 %copy-start.11 = (f32[16,256,8]{1,2,0:T(8,128)S(1)}, f32[16,256,8]{1,2,0:T(8,128)}, u32[]{:S(2)}) copy-start(f32[16,256,8]{1,2,0:T(8,128)} %copy.210) | copy-start | bytes 393220
  422.7 10.2 %copy-start.4 = (f32[16,256,8,64]{1,3,2,0:T(8,128)S(1)}, f32[16,256,8,64]{1,3,2,0:T(8,128)}, u32[]{:S(2)}) copy-start(f32[16,256,8,64]{1,3,2,0:T(8,128)} %copy.212) | copy-start | bytes 25165828
  561.1 2.0 copy-start.3
  564.0 3.4 copy-start.15
  567.4 8.7 %copy-start.1 = (bf16[1,512,2048]{2,1,0:T(8,128)(2,1)S(1)}, bf16[1,512,2048]{2,1,0:T(8,128)(2,1)}, u32[]{:S(2)}) copy-start(bf16[1,512,2048]{2,1,0:T(8,128)(2,1)} %param.11) | copy-start | bytes 6291460
Sparse Core Ops, SparseCore 0:
  8.9 134.2 all-gather.1
